TPU v7x, 32 devices: a whole 2x2x4 slice. The times are simulated.
32 devices in a mesh: seq: 16 (over z, x, core), row: 2 (over y).
Axes of the slice: x: 2, y: 2, z: 4, core: 2. Of those that a mesh axis runs over, the one named last changes fastest.
Arguments:
- patch_queries: bfloat16 [2048, 2048], P('seq', 'row'), may hold values from -15 to 15
- patch_keys: bfloat16 [2048, 2048], P('seq', 'row'), may hold values from -15 to 15
- patch_values: bfloat16 [2048, 2048], P('seq', 'row'), may hold values from -6 to 6
- patch_tasks: int32 [2048], P('seq'), may hold values from 0 to 7
- residual: bfloat16 [2048, 2048], P('seq', 'row'), may hold values from -6 to 6
- output_weight: bfloat16 [2048, 2048], P('row'), may hold values from -0.5 to 0.5
- global_down: bfloat16 [2048, 16], P('row'), may hold values from -0.5 to 0.5
- global_up: bfloat16 [16, 2048], P(None, 'row'), may hold values from -1.5 to 1.5
- global_scales: float32 [8, 16], replicated, may hold values from 0.25 to 4
- local_weight: bfloat16 [2048, 512], P('row'), may hold values from -0.125 to 0.125
- byte_ids: int32 [16384], P('seq'), may hold values from 0 to 255
- byte_table: bfloat16 [256, 512], replicated, may hold values from -6 to 6
- position_table: bfloat16 [8, 512], replicated, may hold values from -6 to 6
- norm_gain: float32 [512], replicated, may hold values from 0.5 to 1.5
- hidden_in: bfloat16 [2048, 512], P('row', 'seq'), may hold values from -0.25 to 0.25
- hidden_out: bfloat16 [2048, 512], P('row', 'seq'), may hold values from -0.125 to 0.125
- local_down: bfloat16 [512, 16], replicated, may hold values from -0.25 to 0.25
- local_up: bfloat16 [16, 2048], P(None, 'row'), may hold values from -1.5 to 1.5
- local_scales: float32 [8, 16], replicated, may hold values from 0.25 to 4
- cotangent: bfloat16 [16384, 512], P(('seq', 'row')), may hold values from -6 to 6
Outputs:
- grad_global_down: float32 [2048, 16], P('row')
- grad_global_up: float32 [16, 2048], P(None, 'row')
- grad_global_scales: float32 [8, 16], replicated
- grad_local_down: float32 [512, 16], replicated
- grad_local_up: float32 [16, 2048], P(None, 'row')
- grad_local_scales: float32 [8, 16], replicated
All inputs are finite; a program needn't handle non-finite values.
Results may differ from a plain program's by a relative error of at most 0.028.
Values may be sent and summed in bfloat16 or wider, within the bound.
A program may use at most 64 MiB of HBM per device.

v0:
```python
import math
import jax
import jax.numpy as jnp
from jax import lax
from jax.sharding import PartitionSpec as P

HEAD = 128
VOCAB = 256
PATCH = 8
TASKS = 8


def contract(left, right, left_dim, right_dim):
    return lax.dot_general(
        left, right, (((left_dim,), (right_dim,)), ((), ())), preferred_element_type=jnp.float32
    )


def select_rows(table, tasks):
    picks = (tasks[:, None] == jnp.arange(table.shape[0], dtype=jnp.int32)[None, :]).astype(
        jnp.float32
    )
    return jnp.dot(picks, table, precision=lax.Precision.HIGHEST)


def task_totals(tasks, values):
    picks = (tasks[:, None] == jnp.arange(TASKS, dtype=jnp.int32)[None, :]).astype(jnp.float32)
    return lax.dot_general(picks, values, (((0,), (0,)), ((), ())), precision=lax.Precision.HIGHEST)


def gelu_slope(upper):
    cumulative = 0.5 * (1.0 + lax.erf(upper * 0.7071067811865476))
    density = jnp.exp(-0.5 * upper * upper) * 0.3989422804014327
    return cumulative + upper * density


def local_inputs(
    identities, projected, tasks, byte_table, position_table, norm_gain, local_down, local_scales
):
    count = identities.shape[0]
    picks = (identities[:, None] == jnp.arange(VOCAB, dtype=jnp.int32)[None, :]).astype(
        jnp.bfloat16
    )
    embedded = jnp.dot(picks, byte_table, preferred_element_type=jnp.float32)
    patches = count // PATCH
    inputs = (
        embedded.reshape(patches, PATCH, -1)
        + position_table.astype(jnp.float32)[None]
        + projected.astype(jnp.float32)[:, None, :]
    )
    inputs = inputs.reshape(count, -1)
    inverse = lax.rsqrt(jnp.mean(inputs * inputs, axis=1, keepdims=True) + 1e-06)
    normed = (inputs * inverse * norm_gain).astype(jnp.bfloat16)
    lowered = jnp.dot(normed, local_down, preferred_element_type=jnp.float32)
    byte_tasks = jnp.repeat(tasks, PATCH)
    scales = select_rows(local_scales, byte_tasks)
    shrunk = (lowered * scales).astype(jnp.bfloat16)
    return (inputs, inverse, normed, lowered, scales, shrunk, byte_tasks)


def keep_state(current):
    return current


def update_state(state, query_rows, first, key_heads, value_heads, key_places, scale):
    running_max, running_sum, running_out = state
    count = query_rows.shape[0]
    heads = key_heads.shape[1]
    query_heads = query_rows.reshape(count, heads, HEAD)
    scores = (
        jnp.einsum("qhd,khd->hqk", query_heads, key_heads, preferred_element_type=jnp.float32)
        * scale
    )
    query_places = first + jnp.arange(count, dtype=jnp.int32)
    allowed = key_places[None, :] <= query_places[:, None]
    scores = jnp.where(allowed[None], scores, -1e30)
    new_max = jnp.maximum(running_max, jnp.max(scores, axis=2))
    weights = jnp.where(allowed[None], jnp.exp(scores - new_max[:, :, None]), 0.0)
    shrink = jnp.exp(running_max - new_max)
    running_sum = running_sum * shrink + jnp.sum(weights, axis=2)
    mixed = jnp.einsum(
        "hqk,khd->qhd",
        weights.astype(jnp.bfloat16),
        value_heads,
        preferred_element_type=jnp.float32,
    )
    running_out = running_out * jnp.transpose(shrink)[:, :, None] + mixed
    return (new_max, running_sum, running_out)


def finish_state(state):
    running_max, running_sum, running_out = state
    result = running_out / jnp.transpose(running_sum)[:, :, None]
    return result.reshape(result.shape[0], -1).astype(jnp.bfloat16)


def body(
    patch_queries,
    patch_keys,
    patch_values,
    patch_tasks,
    residual,
    output_weight,
    global_down,
    global_up,
    global_scales,
    local_weight,
    byte_ids,
    byte_table,
    position_table,
    norm_gain,
    hidden_in,
    hidden_out,
    local_down,
    local_up,
    local_scales,
    cotangent,
):
    rows = patch_queries.shape[0]
    width = patch_queries.shape[1]
    heads = width // HEAD
    row_count = lax.axis_size("row")
    seq_index = lax.axis_index("seq")
    row_index = lax.axis_index("row")
    scale = 1.0 / math.sqrt(HEAD)
    own_first = seq_index * rows
    groups = [(patch_queries, own_first)]

    def visit(state, query_rows, first, key_heads, value_heads, key_places):

        def refresh(current):
            return update_state(
                current, query_rows, first, key_heads, value_heads, key_places, scale
            )

        return lax.cond(
            key_places[0] <= first + query_rows.shape[0] - 1, refresh, keep_state, state
        )

    initial = tuple(
        (
            (
                jnp.full((heads, query_rows.shape[0]), -1e30, jnp.float32),
                jnp.zeros((heads, query_rows.shape[0]), jnp.float32),
                jnp.zeros((query_rows.shape[0], heads, HEAD), jnp.float32),
            )
            for query_rows, first in groups
        )
    )
    key_piece = lax.all_gather(patch_keys, "seq", axis=0, tiled=True)
    value_piece = lax.all_gather(patch_values, "seq", axis=0, tiled=True)
    count = key_piece.shape[0]
    span = math.gcd(count, 1024)

    def one_span(index, states):
        offset = index * span
        key_heads = lax.dynamic_slice_in_dim(key_piece, offset, span, 0).reshape(span, heads, HEAD)
        value_heads = lax.dynamic_slice_in_dim(value_piece, offset, span, 0).reshape(
            span, heads, HEAD
        )
        key_places = offset + jnp.arange(span, dtype=jnp.int32)
        updated = []
        for (query_rows, first), state in zip(groups, states):
            updated.append(visit(state, query_rows, first, key_heads, value_heads, key_places))
        return tuple(updated)

    states = lax.fori_loop(0, count // span, one_span, initial)
    outputs = [finish_state(state) for state in states]
    attended = outputs[0]
    reduced = lax.psum(jnp.dot(attended, global_down, preferred_element_type=jnp.float32), "row")
    task_scales = select_rows(global_scales, patch_tasks)
    scaled = (reduced * task_scales).astype(jnp.bfloat16)
    mixed = lax.psum_scatter(
        contract(output_weight, attended, 0, 1).astype(jnp.bfloat16),
        "row",
        scatter_dimension=0,
        tiled=True,
    ).astype(jnp.float32)
    mixed = mixed + jnp.transpose(residual.astype(jnp.float32)) + contract(global_up, scaled, 0, 1)
    mixed_b = mixed.astype(jnp.bfloat16)
    own_patches = rows // row_count
    own_bytes = own_patches * PATCH
    rows_in, rows_out = (
        lax.all_gather(hidden_in, "seq", axis=1, tiled=True),
        lax.all_gather(hidden_out, "seq", axis=1, tiled=True),
    )
    partial_value = contract(mixed_b, local_weight, 0, 0)
    projected = lax.psum(partial_value.astype(jnp.bfloat16), "row")
    every = local_inputs(
        byte_ids,
        projected,
        patch_tasks,
        byte_table,
        position_table,
        norm_gain,
        local_down,
        local_scales,
    )
    normed_all = every[2]
    shrunk_all = every[5]
    cotangent_all = lax.all_gather(cotangent, "row", axis=0, tiled=True)
    inputs, inverse, normed, lowered, scales, shrunk, byte_tasks = [
        lax.dynamic_slice_in_dim(value, row_index * own_bytes, own_bytes, 0) for value in every
    ]
    upper = contract(normed_all, rows_in, 1, 1) + jnp.dot(
        shrunk_all, local_up, preferred_element_type=jnp.float32
    )
    through = contract(cotangent_all, rows_out, 1, 1)
    grown = (through * gelu_slope(upper)).astype(jnp.bfloat16)
    grad_local_up = contract(shrunk_all, grown, 0, 0)
    back_norm, back_rank = (
        lax.psum_scatter(
            jnp.dot(grown, rows_in, preferred_element_type=jnp.float32).astype(jnp.bfloat16),
            "row",
            scatter_dimension=0,
            tiled=True,
        ).astype(jnp.float32),
        lax.psum_scatter(
            contract(grown, local_up, 1, 1).astype(jnp.bfloat16),
            "row",
            scatter_dimension=0,
            tiled=True,
        ).astype(jnp.float32),
    )
    grad_local_scales = task_totals(byte_tasks, back_rank * lowered)
    moved = (back_rank * scales).astype(jnp.bfloat16)
    grad_local_down = contract(normed, moved, 0, 0)
    back_total = back_norm + contract(moved, local_down, 1, 1)
    gained = back_total * norm_gain
    average = jnp.mean(gained * inputs, axis=1, keepdims=True)
    back_inputs = cotangent.astype(jnp.float32) + inverse * (
        gained - inputs * inverse * inverse * average
    )
    patch_grad = back_inputs.reshape(own_patches, PATCH, -1).sum(axis=1).astype(jnp.bfloat16)
    back_mixed = contract(
        lax.all_gather(patch_grad, "row", axis=0, tiled=True), local_weight, 1, 1
    ).astype(jnp.bfloat16)
    grad_global_up = contract(scaled, back_mixed, 0, 0)
    back_scaled = lax.psum(contract(back_mixed, global_up, 1, 1), "row")
    grad_global_scales = task_totals(patch_tasks, back_scaled * reduced)
    back_reduced = (back_scaled * task_scales).astype(jnp.bfloat16)
    grad_global_down = contract(attended, back_reduced, 0, 0)
    grad_global_down, grad_global_up, grad_global_scales, grad_local_up = lax.psum(
        (grad_global_down, grad_global_up, grad_global_scales, grad_local_up), "seq"
    )
    grad_local_down, grad_local_scales = lax.psum(
        (grad_local_down, grad_local_scales), ("seq", "row")
    )
    return (
        grad_global_down,
        grad_global_up,
        grad_global_scales,
        grad_local_down,
        grad_local_up,
        grad_local_scales,
    )


def solution(mesh):
    placed = (
        P("seq", "row"),
        P("seq", "row"),
        P("seq", "row"),
        P("seq"),
        P("seq", "row"),
        P("row", None),
        P("row", None),
        P(None, "row"),
        P(),
        P("row", None),
        P("seq"),
        P(),
        P(),
        P(),
        P("row", "seq"),
        P("row", "seq"),
        P(),
        P(None, "row"),
        P(),
        P(("seq", "row"), None),
    )
    return jax.shard_map(
        body,
        mesh=mesh,
        in_specs=placed,
        out_specs=(P("row", None), P(None, "row"), P(), P(), P(None, "row"), P()),
        check_vma=False,
    )
```

profile of v0, /device:TPU:0, one launch (start us, length us, event | category | flops | bytes accessed | tf_op | source)
XLA Modules:
  0.0 456.6 jit_solution(17964355863576185190)
XLA Ops:
  7.2 1.9 copy.32
  9.2 1.8 copy.33
  11.1 54.3 %all-gather.6.cloned.1.call-done = bf16[2048,1024]{0,1:T(8,128)(2,1)} async-done(((bf16[128,1024]{0,1:T(8,128)(2,1)}), bf16[2048,1024]{0,1:T(8,128)(2,1)}) %all-gather.6.cloned.1.call-update) | async-done | bytes 4194320 | tf_op jit(solution)/shard_map/all_gather | solution.py:150
  65.4 52.8 %all-gather.8.cloned.1.call-done = bf16[2048,1024]{0,1:T(8,128)(2,1)} async-done(((bf16[128,1024]{0,1:T(8,128)(2,1)}), bf16[2048,1024]{0,1:T(8,128)(2,1)}) %all-gather.8.cloned.1.call-update) | async-done | bytes 4194320 | tf_op jit(solution)/shard_map/all_gather | solution.py:151
  118.3 9.3 %while.19 = (s32[]{:T(128)}, f32[8,128]{1,0:T(8,128)S(1)}, f32[8,128]{1,0:T(8,128)S(1)}, f32[128,8,128]{2,0,1:T(8,128)S(1)}, s32[]{:T(128)}, /*index=5*/s32[]{:T...) while((s32[]{:T(128)}, f32[8,128]{1,0:T(8,128)S(1)}, ...), condition=%wide.region_5.6_spmd, body=%wide.region_0.5_spmd.sunk | while | flops 550899840 | bytes 28124504 | solution.py:167
  118.3 0.5 slice.10
  119.5 6.9 %conditional.2 = ((f32[8,128]{1,0:T(8,128)S(1)}, f32[8,128]{1,0:T(8,128)S(1)}, f32[128,8,128]{2,0,1:T(8,128)S(1)})) conditional(s32[]{:T(128)} %convert_element_type.155, (f32[8,128]{1,0:T(8,128)S(1)}, f32[8,128]{1,0:T(8,128)S(1)}, f32[128,8,128]{2,0,1:T(8,128)S(1)}) %tuple.65, (s32[1024]{0:T(1024)S(1)}, s32[]{:T(128)}, s32[]{:T(128)}, ...), branch_computations={%region_1.0_spmd, %region_2.4_spmd} | conditional | flops 550898816 | bytes 28120166 | solution.py:136
  119.5 2.7 constant_dynamic-slice_fusion
  122.3 0.2 broadcast_compare_fusion
  122.5 1.1 fusion
  123.6 1.7 fusion.13
  125.3 1.0 fusion.2
  126.4 0.5 slice.10
  127.7 0.2 copy.34
  127.9 0.1 divide_convert_fusion
  128.0 3.7 fusion.29
  131.8 0.5 all-gather.10.cloned.1.call-update
  132.4 0.5 all-gather.12.cloned.1.call-update
  133.0 0.2 fusion.65
  133.1 5.0 %psum.63 = f32[128,16]{0,1:T(8,128)S(1)} all-reduce(f32[128,16]{0,1:T(8,128)S(1)} %fusion.65), channel_id=1, replica_groups=mesh['seq'=16,'row'=2] {'row'}, use_global_device_ids=true, to_apply=%region_7.8 | all-reduce | flops 2048 | bytes 16384 | tf_op jit(solution)/shard_map/psum | solution.py:170
  138.1 0.8 multiply_convert_fusion.3
  139.0 12.6 %reduce-scatter.4.cloned.1.call-done = bf16[1024,128]{0,1:T(8,128)(2,1)} async-done(((bf16[2048,128]{0,1:T(8,128)(2,1)}), bf16[1024,128]{0,1:T(8,128)(2,1)}) %reduce-scatter.4.cloned.1.call-update) | async-done | bytes 262160 | tf_op jit(solution)/shard_map/reduce_scatter | solution.py:173
  151.6 2.1 fusion.34
  153.7 0.7 all-gather.14.cloned.1.call-update
  154.5 0.1 eq.29
  154.6 0.1 eq.32
  154.7 0.5 fusion.40
  155.2 19.1 %all-gather.10.cloned.1.call-done = bf16[1024,512]{1,0:T(8,128)(2,1)} async-done(((bf16[512,512]{1,0:T(8,128)(2,1)}), bf16[1024,512]{1,0:T(8,128)(2,1)}) %all-gather.10.cloned.1.call-update) | async-done | bytes 1048592 | tf_op jit(solution)/shard_map/all_gather | solution.py:201
  174.3 39.9 %all-gather.12.cloned.1.call-done = bf16[1024,512]{0,1:T(8,128)(2,1)} async-done(((bf16[1024,32]{0,1:T(8,128)(2,1)}), bf16[1024,512]{0,1:T(8,128)(2,1)}) %all-gather.12.cloned.1.call-update) | async-done | bytes 1048592 | tf_op jit(solution)/shard_map/all_gather | solution.py:185
  214.2 4.7 %fusion.60 = f32[1024,1024]{1,0:T(8,128)} fusion(bf16[1024,512]{1,0:T(8,128)(2,1)} %all-gather.10.cloned.1.call-done, bf16[1024,512]{0,1:T(8,128)(2,1)} %all-gather.12.cloned.1.call-done), kind=kOutput, calls=%fused_computation.86 | convolution fusion | flops 1073741824 | bytes 6291456 | tf_op jit(solution)/shard_map/dot_general | solution.py:14
  218.9 17.9 %all-reduce.5.cloned.1.call-done = bf16[128,512]{1,0:T(8,128)(2,1)} async-done(((bf16[128,512]{1,0:T(8,128)(2,1)}), bf16[128,512]{1,0:T(8,128)(2,1)}) %all-reduce.5.cloned.1.call-update) | async-done | bytes 131088 | tf_op jit(solution)/shard_map/psum | solution.py:188
  236.8 0.9 convert_element_type.97
  237.7 1.6 multiply_reduce_fusion
  239.4 0.6 copy-done.9
  240.0 0.2 multiply_convert_fusion
  240.2 1.0 copy-done.3
  241.2 1.0 multiply_convert_fusion.1
  242.3 34.6 %all-gather.14.cloned.1.call-done = bf16[1024,512]{0,1:T(8,128)(2,1)} async-done(((bf16[1024,32]{0,1:T(8,128)(2,1)}), bf16[1024,512]{0,1:T(8,128)(2,1)}) %all-gather.14.cloned.1.call-update) | async-done | bytes 1048592 | tf_op jit(solution)/shard_map/all_gather | solution.py:184
  276.8 2.9 fusion.61
  279.8 2.3 fusion.28
  282.1 1.3 copy-done.1
  283.4 1.3 convolution_convert_fusion.3
  284.7 0.2 reduce-scatter.6.cloned.1.call-start
  284.9 4.1 convolution_convert_fusion.1
  289.2 1.3 dynamic_slice.47
  290.5 1.3 dynamic-slice.3
  291.8 2.6 fusion.64
  294.4 1.8 fusion.43
  296.2 1.2 fusion.36
  297.4 40.2 %all-reduce = (f32[512,16]{0,1:T(8,128)}, f32[8,16]{1,0:T(8,128)}) all-reduce(f32[512,16]{0,1:T(8,128)S(1)} %fusion.36, f32[8,16]{1,0:T(8,128)} %fusion.43), channel_id=1, replica_groups=mesh['seq'=16,'row'=2] {'seq','row'}, use_global_device_ids=true, to_apply=%region_18.19 | all-reduce | flops 8320 | bytes 66560 | tf_op jit(solution)/shard_map/psum | solution.py:246
  337.7 1.5 multiply_reduce_fusion.1
  339.2 1.6 bitcast_reduce_fusion
  340.8 5.2 %all_gather.23 = bf16[128,512]{1,0:T(8,128)(2,1)S(1)} all-gather(bf16[64,512]{1,0:T(8,128)(2,1)S(1)} %bitcast_reduce_fusion), channel_id=1, replica_groups=mesh['seq'=16,'row'=2] {'row'}, dimensions={0}, use_global_device_ids=true | all-gather | bytes 196608 | tf_op jit(solution)/shard_map/all_gather | solution.py:236
  346.0 0.5 convolution_convert_fusion.2
  346.5 0.2 fusion.62
  346.7 0.8 fusion.63
  347.5 5.0 %psum.65 = f32[128,16]{0,1:T(8,128)S(1)} all-reduce(f32[128,16]{0,1:T(8,128)S(1)} %fusion.62), channel_id=1, replica_groups=mesh['seq'=16,'row'=2] {'row'}, use_global_device_ids=true, to_apply=%region_14.15 | all-reduce | flops 2048 | bytes 16384 | tf_op jit(solution)/shard_map/psum | solution.py:239
  352.4 0.8 fusion.55
  353.3 0.2 fusion.49
  353.5 30.1 %psum.68 = f32[8,16]{1,0:T(8,128)} all-reduce(f32[8,16]{1,0:T(8,128)S(1)} %fusion.49), channel_id=1, replica_groups=mesh['seq'=16,'row'=2] {'seq'}, use_global_device_ids=true, to_apply=%region_17.18 | all-reduce | flops 128 | bytes 1024 | tf_op jit(solution)/shard_map/psum | solution.py:243
  383.6 61.7 %all-reduce.7.cloned.1.call-done = (f32[1024,16]{0,1:T(8,128)}, f32[16,1024]{1,0:T(8,128)}, f32[16,1024]{1,0:T(8,128)}) async-done(((f32[1024,16]{0,1:T(8,128)}, f32[16,1024]{1,0:T(8,128)}, f32[16,1024]{1,0:T(8,128)}), (f32[1024,16]{0,1:T(8,128)}, f32[16,1024]{1,0:T(8,128)}, f32[16,1024]{1,0:T(8,128)})) %all-reduce.7.cloned.1.call-update) | async-done | bytes 196624 | tf_op jit(solution)/shard_map/psum | solution.py:243
  445.3 1.5 copy.67
  446.8 1.5 copy.68
  448.3 1.5 copy.69
  (74 shorter events, 0.7 us)
Async XLA Ops:
  7.2 144.4 %copy-start = (bf16[1024,512]{1,0:T(8,128)(2,1)S(1)}, bf16[1024,512]{1,0:T(8,128)(2,1)}, u32[]{:S(2)}) copy-start(bf16[1024,512]{1,0:T(8,128)(2,1)} %param.33) | copy-start | bytes 3145732
  7.2 58.2 %all-gather.6.cloned.1.call-start = ((), (), s32[]{:S(2)}) async-start(), calls=%async_computation.3 | async-start | bytes 4456448 | tf_op jit(solution)/shard_map/all_gather | solution.py:150
  9.1 109.1 %all-gather.8.cloned.1.call-start = ((), (), s32[]{:S(2)}) async-start(), calls=%async_computation.4 | async-start | bytes 4456448 | tf_op jit(solution)/shard_map/all_gather | solution.py:151
  11.0 140.6 %reduce-scatter.4.cloned.1.call-start = ((), (), s32[]{:S(2)}) async-start(), calls=%async_computation.5 | async-start | bytes 786432 | tf_op jit(solution)/shard_map/reduce_scatter | solution.py:173
  119.5 3.0 copy-start.2
  127.6 5.3 %copy-start.8 = (bf16[1024,16]{0,1:T(8,128)(2,1)S(1)}, bf16[1024,16]{0,1:T(8,128)(2,1)}, u32[]{:S(2)}) copy-start(bf16[1024,16]{0,1:T(8,128)(2,1)} %param.30) | copy-start | bytes 98308
  127.6 10.5 %copy-start.18 = (s32[128]{0:T(128)S(1)}, s32[128]{0:T(128)}, u32[]{:S(2)}) copy-start(s32[128]{0:T(128)} %param.27) | copy-start | bytes 1540
  127.6 10.5 %copy-start.20 = (f32[8,16]{1,0:T(8,128)S(1)}, f32[8,16]{1,0:T(8,128)}, u32[]{:S(2)}) copy-start(f32[8,16]{1,0:T(8,128)} %param.32) | copy-start | bytes 1540
  127.7 23.9 %copy-start.4 = (bf16[128,1024]{1,0:T(8,128)(2,1)S(1)}, bf16[128,1024]{1,0:T(8,128)(2,1)}, u32[]{:S(2)}) copy-start(bf16[128,1024]{1,0:T(8,128)(2,1)} %param.28) | copy-start | bytes 786436
  127.7 23.9 %copy-start.5 = (bf16[16,1024]{1,0:T(8,128)(2,1)S(1)}, bf16[16,1024]{1,0:T(8,128)(2,1)}, u32[]{:S(2)}) copy-start(bf16[16,1024]{1,0:T(8,128)(2,1)} %param.31) | copy-start | bytes 98308
  127.9 26.5 %copy-start.13 = (bf16[8,512]{1,0:T(8,128)(2,1)S(1)}, bf16[8,512]{1,0:T(8,128)(2,1)}, u32[]{:S(2)}) copy-start(bf16[8,512]{1,0:T(8,128)(2,1)} %param.36) | copy-start | bytes 24580
  128.0 26.7 %copy-start.21 = (f32[8,16]{1,0:T(8,128)S(1)}, f32[8,16]{1,0:T(8,128)}, u32[]{:S(2)}) copy-start(f32[8,16]{1,0:T(8,128)} %param.42) | copy-start | bytes 1540
  131.7 42.6 %all-gather.10.cloned.1.call-start = ((), (), s32[]{:S(2)}) async-start(), calls=%async_computation.7 | async-start | bytes 1572864 | tf_op jit(solution)/shard_map/all_gather | solution.py:201
  132.3 81.9 %all-gather.12.cloned.1.call-start = ((), (), s32[]{:S(2)}) async-start(), calls=%async_computation.8 | async-start | bytes 1114112 | tf_op jit(solution)/shard_map/all_gather | solution.py:185
  132.9 103.9 %all-reduce.5.cloned.1.call-start = ((), (), s32[]{:S(2)}) async-start(), calls=%async_computation.6 | async-start | bytes 262144 | tf_op jit(solution)/shard_map/psum | solution.py:188
  138.1 80.8 %copy-start.15 = (f32[128,16]{0,1:T(8,128)}, f32[128,16]{0,1:T(8,128)S(1)}, u32[]{:S(2)}) copy-start(f32[128,16]{0,1:T(8,128)S(1)} %psum.63) | copy-start | bytes 24580
  139.0 15.6 %copy-start.10 = (bf16[128,16]{0,1:T(8,128)(2,1)}, bf16[128,16]{0,1:T(8,128)(2,1)S(1)}, u32[]{:S(2)}) copy-start(bf16[128,16]{0,1:T(8,128)(2,1)S(1)} %get-tuple-element.359) | copy-start | bytes 12292
  153.7 123.2 %all-gather.14.cloned.1.call-start = ((), (), s32[]{:S(2)}) async-start(), calls=%async_computation.9 | async-start | bytes 1114112 | tf_op jit(solution)/shard_map/all_gather | solution.py:184
  154.4 140.0 %reduce-scatter.8.cloned.1.call-start = ((), (), s32[]{:S(2)}) async-start(), calls=%async_computation.11 | async-start | bytes 49152 | tf_op jit(solution)/shard_map/reduce_scatter | solution.py:218
  154.7 64.2 %copy-start.12 = (s32[1024]{0:T(1024)}, s32[1024]{0:T(1024)S(1)}, u32[]{:S(2)}) copy-start(s32[1024]{0:T(1024)S(1)} %eq.32) | copy-start | bytes 12292
  155.2 84.8 %copy-start.17 = (f32[512]{0:T(512)S(1)}, f32[512]{0:T(512)}, u32[]{:S(2)}) copy-start(f32[512]{0:T(512)} %param.37) | copy-start | bytes 6148
  218.9 22.3 %copy-start.6 = (bf16[512,16]{0,1:T(8,128)(2,1)S(1)}, bf16[512,16]{0,1:T(8,128)(2,1)}, u32[]{:S(2)}) copy-start(bf16[512,16]{0,1:T(8,128)(2,1)} %param.40) | copy-start | bytes 49156
  239.4 0.6 copy-start.9
  240.2 1.0 copy-start.3
  276.8 3.0 copy-start.7
  276.8 3.0 copy-start.22
  282.1 1.3 copy-start.1
  284.7 52.9 %reduce-scatter.6.cloned.1.call-start = ((), (), s32[]{:S(2)}) async-start(), calls=%async_computation.10 | async-start | bytes 1572864 | tf_op jit(solution)/shard_map/reduce_scatter | solution.py:212
  289.1 156.2 %all-reduce.7.cloned.1.call-start = ((), (), s32[]{:S(2)}) async-start(), calls=%async_computation.12 | async-start | bytes 393216 | tf_op jit(solution)/shard_map/psum | solution.py:243
  337.6 9.0 %copy-start.11 = (bf16[128,16]{0,1:T(8,128)(2,1)S(1)}, bf16[128,16]{0,1:T(8,128)(2,1)}, u32[]{:S(2)}) copy-start(bf16[128,16]{0,1:T(8,128)(2,1)} %copy-done.10) | copy-start | bytes 12292
  337.6 14.8 %copy-start.14 = (f32[128,16]{0,1:T(8,128)S(1)}, f32[128,16]{0,1:T(8,128)}, u32[]{:S(2)}) copy-start(f32[128,16]{0,1:T(8,128)} %get-tuple-element.360) | copy-start | bytes 24580
  337.6 15.7 %copy-start.16 = (f32[128,16]{0,1:T(8,128)S(1)}, f32[128,16]{0,1:T(8,128)}, u32[]{:S(2)}) copy-start(f32[128,16]{0,1:T(8,128)} %copy-done.15) | copy-start | bytes 24580
  337.6 15.7 %copy-start.19 = (s32[128]{0:T(128)S(1)}, s32[128]{0:T(128)}, u32[]{:S(2)}) copy-start(s32[128]{0:T(128)} %param.27) | copy-start | bytes 1540
Sparse Core Ops, SparseCore 0:
  10.1 55.1 all-gather.5
  67.5 50.6 all-gather.7
  131.9 19.6 reduce-scatter.3
  153.0 21.2 all-gather.9
  176.3 37.8 all-gather.11
  216.3 20.4 all-reduce.4
  239.0 37.8 all-gather.13
  284.8 8.9 reduce-scatter.7
  296.1 20.9 reduce-scatter.5
  353.4 91.8 all-reduce.6
where the time goes:
time: 457 us
  waiting for transfers between devices  295 us (65%)
  blocking collectives  85.4 us (19%)
  matrix products  37.7 us (8%)
  local copies, waits for them, and re-layouts  17.9 us (4%)
  between operations  14.5 us (3%)
    psum x1, waiting for transfers between devices, body(): lax.psum((grad_global_down, grad_global_up, grad_global_scales, grad_loca...  61.7 us
    all_gather x1, waiting for transfers between devices, body(): key_piece = lax.all_gather(patch_keys, 'seq', axis=0, tiled=True)  54.3 us
    all_gather x1, waiting for transfers between devices, body(): value_piece = lax.all_gather(patch_values, 'seq', axis=0, tiled=True)  52.8 us
    psum x1, blocking collectives, body(): lax.psum((grad_local_down, grad_local_scales), ('seq', 'row'))  40.2 us
    all_gather x1, waiting for transfers between devices, body(): lax.all_gather(hidden_out, 'seq', axis=1, tiled=True)  39.9 us
    all_gather x1, waiting for transfers between devices, body(): lax.all_gather(hidden_in, 'seq', axis=1, tiled=True)  34.6 us
    psum x1, blocking collectives, body(): lax.psum((grad_global_down, grad_global_up, grad_global_scales, grad_loca...  30.1 us
    dot_general x12, matrix products, contract(): lax.dot_general(left, right, (((left_dim,), (right_dim,)), ((), ())), pre...  22.4 us
  transfers between devices with their start and end apart: 10, of which 8 were waited for; matrix products, arithmetic and copies ran while one was open for 6% of the time, Pallas kernels for 0%

commit v1 on v0

--- a/solution.py
+++ b/solution.py
@@ -8,6 +8,14 @@
 VOCAB = 256
 PATCH = 8
 TASKS = 8
+
+
+def slabs_advance(inner_x, v0, mesh_dim):
+    return jnp.split(
+        lax.all_gather(jnp.concatenate([inner_x, v0], axis=1), mesh_dim, axis=0, tiled=True),
+        [inner_x.shape[1]],
+        axis=1,
+    )
 
 
 def contract(left, right, left_dim, right_dim):
@@ -147,8 +155,7 @@
             for query_rows, first in groups
         )
     )
-    key_piece = lax.all_gather(patch_keys, "seq", axis=0, tiled=True)
-    value_piece = lax.all_gather(patch_values, "seq", axis=0, tiled=True)
+    key_piece, value_piece = slabs_advance(patch_keys, patch_values, "seq")
     count = key_piece.shape[0]
     span = math.gcd(count, 1024)
 

time: 457 us -> 436 us (0.954)
  waiting for transfers between devices: 295 us -> 268 us
  local copies, waits for them, and re-layouts: 17.9 us -> 22.5 us
    all_gather x2 -> x1, waiting for transfers between devices: 107 us -> 80.5 us  [slabs_advance(): lax.all_gather(jnp.concatenate([inner_x, v0], axis=1), mesh_dim, axis=0,...]
    split x0 -> x1, local copies, waits for them, and re-layouts: none -> 6.02 us  [slabs_advance(): jnp.split(lax.all_gather(jnp.concatenate([inner_x, v0], axis=1), mesh_dim...]
    unnamed x49 -> x51, local copies, waits for them, and re-layouts: 11.1 us -> 9.72 us
  transfers between devices with their start and end apart: 10 -> 9, of which waited for: 8 -> 7; matrix products, arithmetic and copies ran while one was open for 6% -> 6% of each run, Pallas kernels for 0% -> 0%
where the time goes in v1:
time: 436 us; the launch traced here: 435 us
  waiting for transfers between devices  268 us (61%)
  blocking collectives  85.4 us (20%)
  matrix products  37.7 us (9%)
  local copies, waits for them, and re-layouts  22.5 us (5%)
  between operations  14.2 us (3%)
  other arithmetic  5 us (1%)
    all_gather x1, waiting for transfers between devices, slabs_advance(): lax.all_gather(jnp.concatenate([inner_x, v0], axis=1), mesh_dim, axis=0,...  80.5 us
    psum x1, waiting for transfers between devices, body(): lax.psum((grad_global_down, grad_global_up, grad_global_scales, grad_loca...  61.8 us
    psum x1, blocking collectives, body(): lax.psum((grad_local_down, grad_local_scales), ('seq', 'row'))  40.2 us
    all_gather x1, waiting for transfers between devices, body(): lax.all_gather(hidden_out, 'seq', axis=1, tiled=True)  39.9 us
    all_gather x1, waiting for transfers between devices, body(): lax.all_gather(hidden_in, 'seq', axis=1, tiled=True)  34.5 us
    psum x1, blocking collectives, body(): lax.psum((grad_global_down, grad_global_up, grad_global_scales, grad_loca...  30.1 us
    dot_general x12, matrix products, contract(): lax.dot_general(left, right, (((left_dim,), (right_dim,)), ((), ())), pre...  22.4 us
    all_gather x1, waiting for transfers between devices, body(): cotangent_all = lax.all_gather(cotangent, 'row', axis=0, tiled=True)  19.3 us
  transfers between devices with their start and end apart: 9, of which 7 were waited for; matrix products, arithmetic and copies ran while one was open for 6% of the time, Pallas kernels for 0%

profile of v1, /device:TPU:0, one launch (start us, length us, event | category | flops | bytes accessed | tf_op | source)
XLA Modules:
  0.0 434.9 jit_solution(17133954023818256263)
XLA Ops:
  7.2 1.2 copy.32
  8.4 1.1 copy.33
  9.6 0.9 pad_maximum_fusion
  10.5 80.5 %all-gather.5.cloned.1.call-done = bf16[2048,2048]{0,1:T(8,128)(2,1)} async-done(((bf16[128,2048]{0,1:T(8,128)(2,1)}), bf16[2048,2048]{0,1:T(8,128)(2,1)}) %all-gather.5.cloned.1.call-update) | async-done | bytes 8388624 | tf_op jit(solution)/shard_map/all_gather | solution.py:15
  91.1 6.0 %fusion.60 = (bf16[2048,1024]{0,1:T(8,128)(2,1)}, bf16[2048,1024]{0,1:T(8,128)(2,1)}) fusion(bf16[2048,2048]{0,1:T(8,128)(2,1)} %all-gather.5.cloned.1.call-done), kind=kLoop, calls=%fused_computation.87 | loop fusion | bytes 16777216 | tf_op jit(solution)/shard_map/split | solution.py:14
  97.2 9.3 %while.19 = (s32[]{:T(128)}, f32[8,128]{1,0:T(8,128)S(1)}, f32[8,128]{1,0:T(8,128)S(1)}, f32[128,8,128]{2,0,1:T(8,128)S(1)}, s32[]{:T(128)}, /*index=5*/s32[]{:T...) while((s32[]{:T(128)}, f32[8,128]{1,0:T(8,128)S(1)}, ...), condition=%wide.region_5.6_spmd, body=%wide.region_0.5_spmd.sunk | while | flops 550899840 | bytes 27075900 | solution.py:174
  97.2 0.5 slice.10
  98.3 6.8 %conditional.2 = ((f32[8,128]{1,0:T(8,128)S(1)}, f32[8,128]{1,0:T(8,128)S(1)}, f32[128,8,128]{2,0,1:T(8,128)S(1)})) conditional(s32[]{:T(128)} %convert_element_type.155, (f32[8,128]{1,0:T(8,128)S(1)}, f32[8,128]{1,0:T(8,128)S(1)}, f32[128,8,128]{2,0,1:T(8,128)S(1)}) %tuple.66, (s32[1024]{0:T(1024)S(1)}, s32[]{:T(128)}, s32[]{:T(128)}, ...), branch_computations={%region_1.0_spmd, %region_2.4_spmd} | conditional | flops 550898816 | bytes 27071562 | solution.py:144
  98.4 2.7 constant_dynamic-slice_fusion
  101.1 0.2 broadcast_compare_fusion
  101.3 1.2 fusion
  102.4 1.7 fusion.13
  104.1 1.0 fusion.2
  105.2 0.5 slice.10
  106.5 0.2 copy.34
  106.8 3.8 fusion.29
  110.6 0.7 all-gather.7.cloned.1.call-update
  111.3 0.5 all-gather.9.cloned.1.call-update
  111.9 0.2 fusion.66
  112.1 5.0 %psum.63 = f32[128,16]{0,1:T(8,128)S(1)} all-reduce(f32[128,16]{0,1:T(8,128)S(1)} %fusion.66), channel_id=1, replica_groups=mesh['seq'=16,'row'=2] {'row'}, use_global_device_ids=true, to_apply=%region_7.8 | all-reduce | flops 2048 | bytes 16384 | tf_op jit(solution)/shard_map/psum | solution.py:177
  117.1 0.9 multiply_convert_fusion.3
  117.9 12.4 %reduce-scatter.4.cloned.1.call-done = bf16[1024,128]{0,1:T(8,128)(2,1)} async-done(((bf16[2048,128]{0,1:T(8,128)(2,1)}), bf16[1024,128]{0,1:T(8,128)(2,1)}) %reduce-scatter.4.cloned.1.call-update) | async-done | bytes 262160 | tf_op jit(solution)/shard_map/reduce_scatter | solution.py:180
  130.3 2.1 fusion.34
  132.5 0.5 all-gather.11.cloned.1.call-update
  133.0 0.2 reduce-scatter.8.cloned.1.call-start
  133.2 0.1 eq.29
  133.3 0.1 eq.32
  133.4 0.5 fusion.40
  133.9 19.3 %all-gather.7.cloned.1.call-done = bf16[1024,512]{1,0:T(8,128)(2,1)} async-done(((bf16[512,512]{1,0:T(8,128)(2,1)}), bf16[1024,512]{1,0:T(8,128)(2,1)}) %all-gather.7.cloned.1.call-update) | async-done | bytes 1048592 | tf_op jit(solution)/shard_map/all_gather | solution.py:208
  153.2 39.9 %all-gather.9.cloned.1.call-done = bf16[1024,512]{0,1:T(8,128)(2,1)} async-done(((bf16[1024,32]{0,1:T(8,128)(2,1)}), bf16[1024,512]{0,1:T(8,128)(2,1)}) %all-gather.9.cloned.1.call-update) | async-done | bytes 1048592 | tf_op jit(solution)/shard_map/all_gather | solution.py:192
  193.1 4.7 %fusion.61 = f32[1024,1024]{1,0:T(8,128)} fusion(bf16[1024,512]{1,0:T(8,128)(2,1)} %all-gather.7.cloned.1.call-done, bf16[1024,512]{0,1:T(8,128)(2,1)} %all-gather.9.cloned.1.call-done), kind=kOutput, calls=%fused_computation.88 | convolution fusion | flops 1073741824 | bytes 6291456 | tf_op jit(solution)/shard_map/dot_general | solution.py:22
  197.8 17.9 %all-reduce.5.cloned.1.call-done = bf16[128,512]{1,0:T(8,128)(2,1)} async-done(((bf16[128,512]{1,0:T(8,128)(2,1)}), bf16[128,512]{1,0:T(8,128)(2,1)}) %all-reduce.5.cloned.1.call-update) | async-done | bytes 131088 | tf_op jit(solution)/shard_map/psum | solution.py:195
  215.7 0.9 convert_element_type.97
  216.6 1.6 multiply_reduce_fusion
  218.3 0.6 copy-done.9
  218.9 0.2 multiply_convert_fusion
  219.1 1.0 copy-done.3
  220.1 1.0 multiply_convert_fusion.1
  221.1 34.5 %all-gather.11.cloned.1.call-done = bf16[1024,512]{0,1:T(8,128)(2,1)} async-done(((bf16[1024,32]{0,1:T(8,128)(2,1)}), bf16[1024,512]{0,1:T(8,128)(2,1)}) %all-gather.11.cloned.1.call-update) | async-done | bytes 1048592 | tf_op jit(solution)/shard_map/all_gather | solution.py:191
  255.6 2.9 fusion.62
  258.6 2.3 fusion.28
  260.8 1.3 copy-done.1
  262.2 1.3 convolution_convert_fusion.3
  263.5 4.1 convolution_convert_fusion.1
  267.7 1.4 dynamic_slice.47
  269.1 1.3 dynamic-slice.3
  270.4 2.6 fusion.65
  273.0 1.8 fusion.43
  274.8 1.2 fusion.36
  276.0 40.2 %all-reduce = (f32[512,16]{0,1:T(8,128)}, f32[8,16]{1,0:T(8,128)}) all-reduce(f32[512,16]{0,1:T(8,128)S(1)} %fusion.36, f32[8,16]{1,0:T(8,128)} %fusion.43), channel_id=1, replica_groups=mesh['seq'=16,'row'=2] {'seq','row'}, use_global_device_ids=true, to_apply=%region_18.19 | all-reduce | flops 8320 | bytes 66560 | tf_op jit(solution)/shard_map/psum | solution.py:253
  316.2 1.5 multiply_reduce_fusion.1
  317.8 1.6 bitcast_reduce_fusion
  319.4 5.2 %all_gather.19 = bf16[128,512]{1,0:T(8,128)(2,1)S(1)} all-gather(bf16[64,512]{1,0:T(8,128)(2,1)S(1)} %bitcast_reduce_fusion), channel_id=1, replica_groups=mesh['seq'=16,'row'=2] {'row'}, dimensions={0}, use_global_device_ids=true | all-gather | bytes 196608 | tf_op jit(solution)/shard_map/all_gather | solution.py:243
  324.6 0.5 convolution_convert_fusion.2
  325.1 0.2 fusion.63
  325.2 0.8 fusion.64
  326.0 5.0 %psum.65 = f32[128,16]{0,1:T(8,128)S(1)} all-reduce(f32[128,16]{0,1:T(8,128)S(1)} %fusion.63), channel_id=1, replica_groups=mesh['seq'=16,'row'=2] {'row'}, use_global_device_ids=true, to_apply=%region_14.15 | all-reduce | flops 2048 | bytes 16384 | tf_op jit(solution)/shard_map/psum | solution.py:246
  331.0 0.8 fusion.55
  331.9 0.2 fusion.49
  332.1 30.1 %psum.68 = f32[8,16]{1,0:T(8,128)} all-reduce(f32[8,16]{1,0:T(8,128)S(1)} %fusion.49), channel_id=1, replica_groups=mesh['seq'=16,'row'=2] {'seq'}, use_global_device_ids=true, to_apply=%region_17.18 | all-reduce | flops 128 | bytes 1024 | tf_op jit(solution)/shard_map/psum | solution.py:250
  362.2 61.8 %all-reduce.7.cloned.1.call-done = (f32[1024,16]{0,1:T(8,128)}, f32[16,1024]{1,0:T(8,128)}, f32[16,1024]{1,0:T(8,128)}) async-done(((f32[1024,16]{0,1:T(8,128)}, f32[16,1024]{1,0:T(8,128)}, f32[16,1024]{1,0:T(8,128)}), (f32[1024,16]{0,1:T(8,128)}, f32[16,1024]{1,0:T(8,128)}, f32[16,1024]{1,0:T(8,128)})) %all-reduce.7.cloned.1.call-update) | async-done | bytes 196624 | tf_op jit(solution)/shard_map/psum | solution.py:250
  424.0 1.5 copy.67
  425.5 1.5 copy.68
  426.9 1.5 copy.69
  (73 shorter events, 0.7 us)
Async XLA Ops:
  7.2 123.2 %copy-start = (bf16[1024,512]{1,0:T(8,128)(2,1)S(1)}, bf16[1024,512]{1,0:T(8,128)(2,1)}, u32[]{:S(2)}) copy-start(bf16[1024,512]{1,0:T(8,128)(2,1)} %param.33) | copy-start | bytes 3145732
  7.2 83.9 %all-gather.5.cloned.1.call-start = ((), (), s32[]{:S(2)}) async-start(), calls=%async_computation.3 | async-start | bytes 8912896 | tf_op jit(solution)/shard_map/all_gather | solution.py:15
  10.5 119.8 %reduce-scatter.4.cloned.1.call-start = ((), (), s32[]{:S(2)}) async-start(), calls=%async_computation.4 | async-start | bytes 786432 | tf_op jit(solution)/shard_map/reduce_scatter | solution.py:180
  10.5 86.6 %copy-start.2 = (bf16[128,1024]{1,0:T(8,128)(2,1)S(1)}, bf16[128,1024]{1,0:T(8,128)(2,1)}, u32[]{:S(2)}) copy-start(bf16[128,1024]{1,0:T(8,128)(2,1)} %param.24) | copy-start | bytes 786436
  106.4 5.5 %copy-start.8 = (bf16[1024,16]{0,1:T(8,128)(2,1)S(1)}, bf16[1024,16]{0,1:T(8,128)(2,1)}, u32[]{:S(2)}) copy-start(bf16[1024,16]{0,1:T(8,128)(2,1)} %param.30) | copy-start | bytes 98308
  106.4 10.6 %copy-start.18 = (s32[128]{0:T(128)S(1)}, s32[128]{0:T(128)}, u32[]{:S(2)}) copy-start(s32[128]{0:T(128)} %param.27) | copy-start | bytes 1540
  106.4 10.6 %copy-start.20 = (f32[8,16]{1,0:T(8,128)S(1)}, f32[8,16]{1,0:T(8,128)}, u32[]{:S(2)}) copy-start(f32[8,16]{1,0:T(8,128)} %param.32) | copy-start | bytes 1540
  106.5 23.9 %copy-start.4 = (bf16[128,1024]{1,0:T(8,128)(2,1)S(1)}, bf16[128,1024]{1,0:T(8,128)(2,1)}, u32[]{:S(2)}) copy-start(bf16[128,1024]{1,0:T(8,128)(2,1)} %param.28) | copy-start | bytes 786436
  106.5 23.9 %copy-start.5 = (bf16[16,1024]{1,0:T(8,128)(2,1)S(1)}, bf16[16,1024]{1,0:T(8,128)(2,1)}, u32[]{:S(2)}) copy-start(bf16[16,1024]{1,0:T(8,128)(2,1)} %param.31) | copy-start | bytes 98308
  106.7 26.5 %copy-start.13 = (bf16[8,512]{1,0:T(8,128)(2,1)S(1)}, bf16[8,512]{1,0:T(8,128)(2,1)}, u32[]{:S(2)}) copy-start(bf16[8,512]{1,0:T(8,128)(2,1)} %param.36) | copy-start | bytes 24580
  106.8 26.7 %copy-start.21 = (f32[8,16]{1,0:T(8,128)S(1)}, f32[8,16]{1,0:T(8,128)}, u32[]{:S(2)}) copy-start(f32[8,16]{1,0:T(8,128)} %param.42) | copy-start | bytes 1540
  110.5 42.7 %all-gather.7.cloned.1.call-start = ((), (), s32[]{:S(2)}) async-start(), calls=%async_computation.6 | async-start | bytes 1572864 | tf_op jit(solution)/shard_map/all_gather | solution.py:208
  111.3 81.8 %all-gather.9.cloned.1.call-start = ((), (), s32[]{:S(2)}) async-start(), calls=%async_computation.7 | async-start | bytes 1114112 | tf_op jit(solution)/shard_map/all_gather | solution.py:192
  111.9 103.9 %all-reduce.5.cloned.1.call-start = ((), (), s32[]{:S(2)}) async-start(), calls=%async_computation.5 | async-start | bytes 262144 | tf_op jit(solution)/shard_map/psum | solution.py:195
  117.0 80.8 %copy-start.15 = (f32[128,16]{0,1:T(8,128)}, f32[128,16]{0,1:T(8,128)S(1)}, u32[]{:S(2)}) copy-start(f32[128,16]{0,1:T(8,128)S(1)} %psum.63) | copy-start | bytes 24580
  117.9 15.4 %copy-start.10 = (bf16[128,16]{0,1:T(8,128)(2,1)}, bf16[128,16]{0,1:T(8,128)(2,1)S(1)}, u32[]{:S(2)}) copy-start(bf16[128,16]{0,1:T(8,128)(2,1)S(1)} %get-tuple-element.361) | copy-start | bytes 12292
  132.4 123.2 %all-gather.11.cloned.1.call-start = ((), (), s32[]{:S(2)}) async-start(), calls=%async_computation.8 | async-start | bytes 1114112 | tf_op jit(solution)/shard_map/all_gather | solution.py:191
  133.0 140.0 %reduce-scatter.8.cloned.1.call-start = ((), (), s32[]{:S(2)}) async-start(), calls=%async_computation.10 | async-start | bytes 49152 | tf_op jit(solution)/shard_map/reduce_scatter | solution.py:225
  133.4 64.4 %copy-start.12 = (s32[1024]{0:T(1024)}, s32[1024]{0:T(1024)S(1)}, u32[]{:S(2)}) copy-start(s32[1024]{0:T(1024)S(1)} %eq.32) | copy-start | bytes 12292
  133.9 85.0 %copy-start.17 = (f32[512]{0:T(512)S(1)}, f32[512]{0:T(512)}, u32[]{:S(2)}) copy-start(f32[512]{0:T(512)} %param.37) | copy-start | bytes 6148
  197.8 22.3 %copy-start.6 = (bf16[512,16]{0,1:T(8,128)(2,1)S(1)}, bf16[512,16]{0,1:T(8,128)(2,1)}, u32[]{:S(2)}) copy-start(bf16[512,16]{0,1:T(8,128)(2,1)} %param.40) | copy-start | bytes 49156
  218.3 0.6 copy-start.9
  219.1 1.0 copy-start.3
  255.6 3.0 copy-start.7
  255.6 3.0 copy-start.22
  260.8 1.3 copy-start.1
  263.5 52.8 %reduce-scatter.6.cloned.1.call-start = ((), (), s32[]{:S(2)}) async-start(), calls=%async_computation.9 | async-start | bytes 1572864 | tf_op jit(solution)/shard_map/reduce_scatter | solution.py:219
  267.7 156.3 %all-reduce.7.cloned.1.call-start = ((), (), s32[]{:S(2)}) async-start(), calls=%async_computation.11 | async-start | bytes 393216 | tf_op jit(solution)/shard_map/psum | solution.py:250
  316.2 9.0 %copy-start.11 = (bf16[128,16]{0,1:T(8,128)(2,1)S(1)}, bf16[128,16]{0,1:T(8,128)(2,1)}, u32[]{:S(2)}) copy-start(bf16[128,16]{0,1:T(8,128)(2,1)} %copy-done.10) | copy-start | bytes 12292
  316.2 14.8 %copy-start.14 = (f32[128,16]{0,1:T(8,128)S(1)}, f32[128,16]{0,1:T(8,128)}, u32[]{:S(2)}) copy-start(f32[128,16]{0,1:T(8,128)} %get-tuple-element.362) | copy-start | bytes 24580
  316.2 15.7 %copy-start.16 = (f32[128,16]{0,1:T(8,128)S(1)}, f32[128,16]{0,1:T(8,128)}, u32[]{:S(2)}) copy-start(f32[128,16]{0,1:T(8,128)} %copy-done.15) | copy-start | bytes 24580
  316.2 15.7 %copy-start.19 = (s32[128]{0:T(128)S(1)}, s32[128]{0:T(128)}, u32[]{:S(2)}) copy-start(s32[128]{0:T(128)} %param.27) | copy-start | bytes 1540
Sparse Core Ops, SparseCore 0:
  10.6 80.4 all-gather.4
  110.7 19.6 reduce-scatter.3
  131.9 21.2 all-gather.6
  155.2 37.8 all-gather.8
  195.2 20.4 all-reduce.4
  217.7 37.8 all-gather.10
  263.6 8.9 reduce-scatter.7
  274.8 20.9 reduce-scatter.5
  332.0 91.9 all-reduce.6
